TPU v7x, 32 devices: a whole 2x2x4 slice. The times are simulated.
32 devices in a mesh: grp: 4 (over x, core), row: 4 (over z), col: 2 (over y).
Axes of the slice: x: 2, y: 2, z: 4, core: 2. Of those that a mesh axis runs over, the one named last changes fastest.
Arguments:
- cover: float32 [4, 12288, 4096], P('grp', 'row', 'col'), may hold values from -4 to 12, as said below
- prior: float32 [4096, 4096], P(('grp', 'row'), 'col'), may hold values from -0.5 to 2, as said below
Outputs:
- cover_out: float32 [4, 12288, 4096], P('grp', 'row', 'col')
- posterior: float32 [4096, 4096], P(('grp', 'row'), 'col')
Inputs may be any that keep to these rules, and one draw needn't show every extreme that they name: `cover`: the first three slots hold a symmetric positive definite matrix of order 12288 in the column-block order of the steps. `prior`: A symmetric positive definite matrix.
All inputs are finite; a program needn't handle non-finite values.
Results may differ from a plain program's by a relative error of at most 0.0001.
Values sent between devices are 32-bit elements; how exact they have to be, the bound alone decides.
No kernel may reach another device: no remote copies, remote signals or barrier semaphores. Data moves between devices by JAX's collectives and lax.ppermute only.
A program may use at most 192 MiB of HBM per device.

v0:
```python
import jax
import jax.numpy as jnp
from jax import lax
from jax.sharding import PartitionSpec as P

M = 12288
B = 256
precise = lax.Precision.HIGHEST


def broadcast(block, axis, source):
    block = jnp.where(lax.axis_index(axis) == source, block, jnp.zeros_like(block))
    return lax.psum(block, axis)


def advance(region, row_ids, block_ids, lower_rows, solved, panel, on_top):
    update = jnp.dot(lower_rows, solved, precision=precise, preferred_element_type=jnp.float32)
    to_right = block_ids > panel
    result = jnp.where((row_ids >= (panel + 1) * B) & to_right, region - update, region)
    own_column = (block_ids[:, :B] == panel) & (row_ids >= panel * B)
    result = jnp.concatenate(
        [jnp.where(own_column, lower_rows, result[:, :B]), result[:, B:]], axis=1
    )
    stripe = jnp.where(on_top & to_right, solved, result[panel * B : (panel + 1) * B])
    return jnp.concatenate([result[: panel * B], stripe, result[(panel + 1) * B :]], axis=0)


def local(cover, prior):
    local_block = cover[0]
    group_idx = lax.axis_index("grp")
    row_idx = lax.axis_index("row")
    col_idx = lax.axis_index("col")
    group_count = lax.axis_size("grp")
    row_count = lax.axis_size("row")
    col_count = lax.axis_size("col")
    local_rows, local_cols = local_block.shape
    prior_rows = prior.shape[0]
    row_ids = (row_idx * local_rows + jnp.arange(local_rows))[:, None]
    col_blocks = col_idx * (local_cols // B) + jnp.arange(local_cols) // B
    block_ids = jnp.where(
        group_idx < group_count - 1, (group_count - 1) * col_blocks + group_idx, M
    )[None, :]
    on_top = row_idx == 0
    first_col = (group_idx * row_count + row_idx) * prior_rows
    posterior = prior
    column_piece = local_block[:, :B]
    row_piece = local_block[0:B]
    panel_col = broadcast(column_piece, ("grp", "col"), 0 * col_count)
    packed = jnp.concatenate([panel_col[0:B], row_piece], axis=1)
    packed = broadcast(packed, "row", 0)
    factor = jnp.linalg.cholesky(packed[:, :B])
    lower_rows = lax.linalg.triangular_solve(
        factor, panel_col, left_side=False, lower=True, transpose_a=True
    )
    solved = lax.linalg.triangular_solve(factor, packed[:, B:], left_side=True, lower=True)
    local_block = advance(local_block, row_ids, block_ids, lower_rows, solved, 0, on_top)
    command_cols = broadcast(solved, "grp", group_count - 1)
    owner_idx = first_col // local_cols
    window = lax.dynamic_slice_in_dim(command_cols, first_col % local_cols, prior_rows, 1)
    command_rows = broadcast(window, "col", owner_idx)
    posterior = posterior - lax.dot_general(
        command_rows,
        command_cols,
        (((0,), (0,)), ((), ())),
        precision=precise,
        preferred_element_type=jnp.float32,
    )
    return (local_block[None], posterior)


def solution(mesh):
    return jax.shard_map(
        local,
        mesh=mesh,
        in_specs=(P("grp", "row", "col"), P(("grp", "row"), "col")),
        out_specs=(P("grp", "row", "col"), P(("grp", "row"), "col")),
        check_vma=False,
    )
```

profile of v0, /device:TPU:0, one launch (start us, length us, event | category | flops | bytes accessed | tf_op | source)
XLA Modules:
  0.0 432.4 jit_solution(17534666749890213730)
XLA Ops:
  7.2 24.7 %copy.4 = f32[1,3072,2048]{1,2,0:T(8,128)} copy(f32[1,3072,2048]{2,1,0:T(8,128)} %param.2) | data formatting | bytes 50331648 | tf_op args[0]
  31.9 3.9 slice_select_fusion.1
  35.8 0.0 all-reduce.8.cloned.1.call-start
  35.9 1.7 slice_bitcast_fusion
  37.6 70.4 %all-reduce.6.cloned.1.call-done = f32[3072,256]{0,1:T(8,128)} async-done(((f32[3072,256]{0,1:T(8,128)}), f32[3072,256]{0,1:T(8,128)}) %all-reduce.6.cloned.1.call-update) | async-done | bytes 3145744 | tf_op jit(solution)/shard_map/psum | solution.py:13
  108.0 1.0 slice.107
  109.0 1.6 maximum_select_fusion
  110.6 0.0 all-reduce.10.cloned.1.call-start
  110.8 94.6 %all-reduce.8.cloned.1.call-done = f32[256,2304]{0,1:T(8,128)} async-done(((f32[256,2304]{0,1:T(8,128)}), f32[256,2304]{0,1:T(8,128)}) %all-reduce.8.cloned.1.call-update) | async-done | bytes 2359312 | tf_op jit(solution)/shard_map/psum | solution.py:13
  205.4 1.0 slice.109
  206.4 0.1 copy.6
  206.5 1.0 fusion.7
  207.5 11.7 %cholesky.50 = f32[128,128]{1,0:T(8,128)S(1)} custom-call(f32[128,128]{1,0:T(8,128)S(1)} %cholesky.118), custom_call_target="Cholesky" | custom-call | tf_op jit(solution)/shard_map/jit(cholesky)/cholesky | solution.py:51
  219.3 9.8 %custom-call.16 = f32[1,128,128]{1,2,0:T(8,128)S(1)} custom-call(f32[1,128,128]{2,1,0:T(8,128)S(1)} %get-tuple-element.29), custom_call_target="InvertDiagBlocksLowerTriangular" | custom-call | tf_op jit(solution)/shard_map/jit(cholesky)/cholesky | solution.py:51
  229.1 0.2 fusion.8
  229.3 0.3 convolution_subtract_fusion.3
  229.6 11.7 %cholesky.105 = f32[128,128]{1,0:T(8,128)S(1)} custom-call(f32[128,128]{1,0:T(8,128)S(1)} %convolution_subtract_fusion.3), custom_call_target="Cholesky" | custom-call | tf_op jit(solution)/shard_map/jit(cholesky)/cholesky | solution.py:51
  241.3 0.1 copy.9
  241.4 0.1 copy.8
  241.5 0.1 copy.7
  241.6 0.7 compare_reduce_fusion.1
  243.7 0.1 triangular_solve.72
  243.7 4.2 while.1
  243.9 0.6 fusion.39
  244.5 1.3 dynamic-slice.7
  245.8 0.1 copy.17
  245.9 0.6 fusion.39
  246.5 1.3 dynamic-slice.7
  247.8 0.1 copy.17
  247.9 19.7 %custom-call.17 = f32[2,128,128]{1,2,0:T(8,128)S(1)} custom-call(f32[2,128,128]{2,1,0:T(8,128)S(1)} %get-tuple-element.9), custom_call_target="InvertDiagBlocksLowerTriangular" | custom-call | tf_op jit(solution)/shard_map/triangular_solve | solution.py:55
  267.6 2.3 fusion.5
  269.9 0.3 copy.11
  270.3 3.5 convolution_subtract_fusion.2
  273.7 1.0 fusion.12
  274.7 1.5 fusion.2
  276.3 1.6 convolution_subtract_fusion
  277.9 1.5 fusion.11
  279.4 27.7 %subtract_select_fusion = f32[3072,2048]{0,1:T(8,128)} fusion(pred[3072]{0:T(1024)(128)(4,1)S(1)} %get-tuple-element.30, pred[2048]{0:T(1024)(128)(4,1)S(1)} %get-tuple-element.32, f32[3072,128]{0,1:T(8,128)S(1)} %fusion.11, f32[3072,128]{0,1:T(8,128)S(1)} %fusion.2, f32[128,2048]{0,1:T(8,128)S(1)} %fusion.12, f32[128,2048]{0,1:T(8,128)S(1)} %copy.11, ...), kind=kOutput, calls=%fused_computation.2 | convolution fusion | flops 19347537920 | bytes 55579648 | tf_op jit(solution)/shard_map/dot_general | solution.py:17
  307.1 8.3 %slice.114 = f32[3072,1792]{0,1:T(8,128)S(1)} slice(f32[3072,2048]{0,1:T(8,128)} %subtract_select_fusion), slice={[0:3072], [256:2048]} | slice | bytes 44040192 | tf_op jit(solution)/shard_map/slice | solution.py:22
  315.4 4.9 %slice_select_fusion = f32[3072,256]{0,1:T(8,128)S(1)} fusion(f32[3072,2048]{0,1:T(8,128)} %subtract_select_fusion, f32[3072,128]{0,1:T(8,128)S(1)} %fusion.11, f32[3072,128]{0,1:T(8,128)S(1)} %fusion.2, pred[3072]{0:T(1024)(128)(4,1)S(1)} %get-tuple-element.31, pred[256]{0:T(512)(128)(4,1)S(1)} %compare_reduce_fusion), kind=kLoop, calls=%fused_computation.8 | loop fusion | flops 2359296 | bytes 9440512 | tf_op jit(solution)/shard_map/jit(_where)/select_n | solution.py:22
  320.4 0.4 copy-done.2
  320.7 3.0 fusion.4
  323.8 1.7 copy-done
  325.6 50.5 %all-reduce.10.cloned.1.call-done = f32[256,2048]{0,1:T(8,128)} async-done(((f32[256,2048]{0,1:T(8,128)}), f32[256,2048]{0,1:T(8,128)}) %all-reduce.10.cloned.1.call-update) | async-done | bytes 2097168 | tf_op jit(solution)/shard_map/psum | solution.py:13
  376.0 1.7 dynamic-slice_select_fusion
  377.7 18.3 %fusion.1 = f32[1,3072,2048]{1,2,0:T(8,128)} fusion(f32[3072,1792]{0,1:T(8,128)} %copy-done, f32[3072,256]{0,1:T(8,128)S(1)} %slice_select_fusion, f32[256,2048]{0,1:T(8,128)} %get-tuple-element.27), kind=kLoop, calls=%fused_computation.5 | loop fusion | flops 31457280 | bytes 52428800 | tf_op jit(solution)/shard_map/broadcast_in_dim | solution.py:68
  396.0 24.9 %copy.13 = f32[1,3072,2048]{2,1,0:T(8,128)} copy(f32[1,3072,2048]{1,2,0:T(8,128)} %fusion.1) | data formatting | bytes 50331648
  420.9 4.9 %convolution_subtract_fusion.1 = f32[256,2048]{1,0:T(8,128)} fusion(f32[256,2048]{1,0:T(8,128)} %param.3, f32[256,256]{0,1:T(8,128)} %all-reduce.12.cloned.1.call-done, f32[256,2048]{0,1:T(8,128)S(1)} %copy-done.4), kind=kOutput, calls=%fused_computation.11 | convolution fusion | flops 1611137024 | bytes 6553600 | tf_op jit(solution)/shard_map/dot_general | solution.py:61
  (33 shorter events, 0.4 us)
Async XLA Ops:
  7.2 100.9 %all-reduce.6.cloned.1.call-start = ((), (), s32[]{:S(2)}) async-start(), calls=%async_computation | async-start | bytes 6291456 | tf_op jit(solution)/shard_map/psum | solution.py:13
  35.8 169.6 %all-reduce.8.cloned.1.call-start = ((), (), s32[]{:S(2)}) async-start(), calls=%async_computation.1 | async-start | bytes 4718592 | tf_op jit(solution)/shard_map/psum | solution.py:13
  110.6 265.5 %all-reduce.10.cloned.1.call-start = ((), (), s32[]{:S(2)}) async-start(), calls=%async_computation.2 | async-start | bytes 4194304 | tf_op jit(solution)/shard_map/psum | solution.py:13
  270.2 9.2 %copy-start.1 = (f32[128,2048]{0,1:T(8,128)}, f32[128,2048]{0,1:T(8,128)S(1)}, u32[]{:S(2)}) copy-start(f32[128,2048]{0,1:T(8,128)S(1)} %copy.11) | copy-start | bytes 3145732
  270.3 4.5 %copy-start.3 = (f32[3072,256]{0,1:T(8,128)S(1)}, f32[3072,256]{0,1:T(8,128)}, u32[]{:S(2)}) copy-start(f32[3072,256]{0,1:T(8,128)} %all-reduce.6.cloned.1.call-done) | copy-start | bytes 9437188
  315.4 10.1 %copy-start = (f32[3072,1792]{0,1:T(8,128)}, f32[3072,1792]{0,1:T(8,128)S(1)}, u32[]{:S(2)}) copy-start(f32[3072,1792]{0,1:T(8,128)S(1)} %slice.114) | copy-start | bytes 66060292
  315.4 5.3 %copy-start.2 = (f32[128,2048]{0,1:T(8,128)S(1)}, f32[128,2048]{0,1:T(8,128)}, u32[]{:S(2)}) copy-start(f32[128,2048]{0,1:T(8,128)} %copy-done.1) | copy-start | bytes 3145732
  325.5 95.4 %all-reduce.12.cloned.1.call-start = ((), (), s32[]{:S(2)}) async-start(), calls=%async_computation.3 | async-start | bytes 524288 | tf_op jit(solution)/shard_map/psum | solution.py:13
  396.0 24.9 %copy-start.4 = (f32[256,2048]{0,1:T(8,128)S(1)}, f32[256,2048]{0,1:T(8,128)}, u32[]{:S(2)}) copy-start(f32[256,2048]{0,1:T(8,128)} %all-reduce.10.cloned.1.call-done) | copy-start | bytes 6291460
Sparse Core Ops, SparseCore 0:
  36.0 72.0 all-reduce.5
  110.7 94.6 all-reduce.7
  325.6 50.3 all-reduce.9
  378.7 23.3 all-reduce.11
where the time goes:
time: 433 us; the launch traced here: 432 us
  waiting for transfers between devices  216 us (50%)
  other arithmetic  88.2 us (20%)
  local copies, waits for them, and re-layouts  68.4 us (16%)
  matrix products  44.5 us (10%)
  between operations  15.3 us (4%)
    psum x4, waiting for transfers between devices, broadcast(): return lax.psum(block, axis)  215 us
    unnamed x12, local copies, waits for them, and re-layouts  51.6 us
    another operation x6, other arithmetic, local(): factor = jnp.linalg.cholesky(packed[:, :B])  34 us
    dot_general x1, matrix products, advance(): jnp.dot(lower_rows, solved, precision=precise, preferred_element_type=jnp...  27.7 us
    another operation x3, other arithmetic, local(): lax.linalg.triangular_solve(factor, packed[:, B:], left_side=True, lower=...  19.7 us
    broadcast_in_dim x1, other arithmetic, local(): return (local_block[None], posterior)  18.3 us
    select_n x4, other arithmetic, broadcast(): jnp.where(lax.axis_index(axis) == source, block, jnp.zeros_like(block))  10.2 us
  transfers between devices with their start and end apart: 4, of which 3 were waited for; matrix products, arithmetic and copies ran while one was open for 10% of the time, Pallas kernels for 0%

commit v1 on v0

--- a/solution.py
+++ b/solution.py
@@ -8,9 +8,15 @@
 precise = lax.Precision.HIGHEST
 
 
+def summed_here(value, axis):
+    blocks = lax.all_gather(value, axis, axis=0, tiled=False)
+    total = blocks.sum(axis=0)
+    return total
+
+
 def broadcast(block, axis, source):
     block = jnp.where(lax.axis_index(axis) == source, block, jnp.zeros_like(block))
-    return lax.psum(block, axis)
+    return summed_here(block, axis)
 
 
 def advance(region, row_ids, block_ids, lower_rows, solved, panel, on_top):

time: 433 us -> 481 us (1.11)
  waiting for transfers between devices: 216 us -> 292 us
  local copies, waits for them, and re-layouts: 68.4 us -> 19.6 us
  blocking collectives: 0 us -> 8.97 us
  other arithmetic: 88.2 us -> 95.4 us
    all_gather x0 -> x3, waiting for transfers between devices: none -> 292 us  [summed_here(): blocks = lax.all_gather(value, axis, axis=0, tiled=False)]
    psum x4 -> x0, waiting for transfers between devices: 215 us -> none  [broadcast(): return lax.psum(block, axis)]
    unnamed x12 -> x7, local copies, waits for them, and re-layouts: 51.6 us -> 0.83 us
    reduce_sum x0 -> x4, other arithmetic: none -> 18.5 us  [summed_here(): total = blocks.sum(axis=0)]
    all_gather x0 -> x1, blocking collectives: none -> 8.97 us  [summed_here(): blocks = lax.all_gather(value, axis, axis=0, tiled=False)]
    broadcast_in_dim x1, other arithmetic: 18.3 us -> 10.3 us  [local(): return (local_block[None], posterior)]
    another operation x3, matrix products: 4.66 us -> 10.7 us  [local(): lax.linalg.triangular_solve(factor, panel_col, left_side=False, lower=Tru...]
  transfers between devices with their start and end apart: 4 -> 3, of which waited for: 3 -> 2; matrix products, arithmetic and copies ran while one was open for 10% -> 14% of each run, Pallas kernels for 0% -> 0%
where the time goes in v1:
time: 481 us; the launch traced here: 480 us
  waiting for transfers between devices  292 us (61%)
  other arithmetic  95.4 us (20%)
  matrix products  48.7 us (10%)
  local copies, waits for them, and re-layouts  19.6 us (4%)
  between operations  15.3 us (3%)
  blocking collectives  8.97 us (2%)
    all_gather x3, waiting for transfers between devices, summed_here(): blocks = lax.all_gather(value, axis, axis=0, tiled=False)  292 us
    another operation x6, other arithmetic, local(): factor = jnp.linalg.cholesky(packed[:, :B])  34 us
    dot_general x1, matrix products, advance(): jnp.dot(lower_rows, solved, precision=precise, preferred_element_type=jnp...  28.7 us
    another operation x3, other arithmetic, local(): lax.linalg.triangular_solve(factor, packed[:, B:], left_side=True, lower=...  19.7 us
    reduce_sum x4, other arithmetic, summed_here(): total = blocks.sum(axis=0)  18.5 us
    another operation x3, matrix products, local(): lax.linalg.triangular_solve(factor, panel_col, left_side=False, lower=Tru...  10.7 us
    broadcast_in_dim x1, other arithmetic, local(): return (local_block[None], posterior)  10.3 us
  transfers between devices with their start and end apart: 3, of which 2 were waited for; matrix products, arithmetic and copies ran while one was open for 14% of the time, Pallas kernels for 0%

profile of v1, /device:TPU:0, one launch (start us, length us, event | category | flops | bytes accessed | tf_op | source)
XLA Modules:
  0.0 480.0 jit_solution(11029405899571831227)
XLA Ops:
  7.2 0.0 all-gather.10.cloned.1.call-start
  7.2 3.8 slice_select_fusion.1
  11.0 0.0 all-gather.10.cloned.1.call-update
  11.0 0.0 all-gather.6.cloned.1.call-start
  11.1 3.1 slice.85
  14.2 124.9 %all-gather.10.cloned.1.call-done = f32[24576,256]{1,0:T(8,128)} async-done(((f32[3072,256]{1,0:T(8,128)}), f32[24576,256]{1,0:T(8,128)}) %all-gather.10.cloned.1.call-update) | async-done | bytes 25165840 | tf_op jit(solution)/shard_map/all_gather | solution.py:12
  139.1 9.5 %reduce_sum.36 = f32[3072,256]{1,0:T(8,128)S(1)} reduce(f32[8,3072,256]{2,1,0:T(8,128)} %bitcast.49, f32[]{:T(128)} %constant.150.clone.1), dimensions={0}, to_apply=%region_0.1 | reduce | flops 5505024 | bytes 28311556 | tf_op jit(solution)/shard_map/reduce_sum | solution.py:13
  148.6 0.0 copy-start.1
  148.6 4.3 maximum_select_fusion
  152.9 0.0 copy-done.1
  152.9 0.0 all-gather.6.cloned.1.call-update
  152.9 0.0 all-gather.8.cloned.1.call-start
  153.0 166.8 %all-gather.6.cloned.1.call-done = f32[4,256,2304]{2,1,0:T(8,128)} async-done(((f32[1,256,2304]{2,1,0:T(8,128)}), f32[4,256,2304]{2,1,0:T(8,128)}) %all-gather.6.cloned.1.call-update) | async-done | bytes 9437200 | tf_op jit(solution)/shard_map/all_gather | solution.py:12
  319.8 4.5 reduce_sum.37
  324.4 0.1 copy.15
  324.6 11.7 %cholesky.50 = f32[128,128]{1,0:T(8,128)S(1)} custom-call(f32[128,128]{1,0:T(8,128)S(1)} %cholesky.118), custom_call_target="Cholesky" | custom-call | tf_op jit(solution)/shard_map/jit(cholesky)/cholesky | solution.py:57
  336.3 9.8 %custom-call.16 = f32[1,128,128]{1,2,0:T(8,128)S(1)} custom-call(f32[1,128,128]{2,1,0:T(8,128)S(1)} %get-tuple-element.23), custom_call_target="InvertDiagBlocksLowerTriangular" | custom-call | tf_op jit(solution)/shard_map/jit(cholesky)/cholesky | solution.py:57
  346.2 0.2 constant_dynamic-update-slice_fusion.1
  346.4 0.3 convolution_subtract_fusion.3
  346.6 11.7 %cholesky.105 = f32[128,128]{1,0:T(8,128)S(1)} custom-call(f32[128,128]{1,0:T(8,128)S(1)} %convolution_subtract_fusion.3), custom_call_target="Cholesky" | custom-call | tf_op jit(solution)/shard_map/jit(cholesky)/cholesky | solution.py:57
  358.4 0.7 compare_reduce_fusion.1
  360.4 0.1 triangular_solve.78
  360.5 4.2 while.1
  360.6 0.7 fusion.38
  361.3 1.3 bitcast_dynamic-update-slice_fusion.2
  362.7 0.7 fusion.38
  363.3 1.3 bitcast_dynamic-update-slice_fusion.2
  364.7 0.0 copy-start.2
  364.7 0.7 copy-done.2
  365.4 19.7 %custom-call.17 = f32[2,128,128]{1,2,0:T(8,128)S(1)} custom-call(f32[2,128,128]{2,1,0:T(8,128)S(1)} %get-tuple-element.9), custom_call_target="InvertDiagBlocksLowerTriangular" | custom-call | tf_op jit(solution)/shard_map/triangular_solve | solution.py:61
  385.0 1.0 fusion.4
  386.1 1.9 convolution_subtract_fusion.2
  388.0 1.1 fusion.11
  389.0 1.5 maximum_select_fusion.2
  390.5 0.0 all-gather.8.cloned.1.call-update
  390.7 4.2 fusion.2
  394.8 3.2 copy.10
  398.1 5.1 %convolution_subtract_fusion = f32[3072,128]{1,0:T(8,128)S(1)} fusion(f32[3072,128]{0,1:T(8,128)} %fusion.2, f32[3072,256]{1,0:T(8,128)} %copy-done.1, f32[256,256]{1,0:T(8,128)} %copy-done.2), kind=kOutput, calls=%fused_computation.7 | convolution fusion | flops 604372992 | bytes 4784128 | tf_op jit(solution)/shard_map/triangular_solve | solution.py:58
  403.2 0.0 copy-start
  403.2 1.4 fusion.10
  404.7 28.7 %subtract_select_fusion = f32[3072,2048]{1,0:T(8,128)} fusion(pred[2048]{0:T(1024)(128)(4,1)S(1)} %fusion.20, pred[3072]{0:T(1024)(128)(4,1)S(1)} %get-tuple-element.26, f32[3072,128]{1,0:T(8,128)S(1)} %fusion.10, f32[3072,128]{1,0:T(8,128)S(1)} %copy-done, f32[128,2048]{1,0:T(8,128)S(1)} %fusion.11, f32[128,2048]{1,0:T(8,128)S(1)} %fusion.4, ...), kind=kOutput, calls=%fused_computation.2 | convolution fusion | flops 19347537920 | bytes 55579648 | tf_op jit(solution)/shard_map/dot_general | solution.py:23
  433.3 8.3 %slice.110 = f32[3072,1792]{1,0:T(8,128)S(1)} slice(f32[3072,2048]{1,0:T(8,128)} %subtract_select_fusion), slice={[0:3072], [256:2048]} | slice | bytes 44040192 | tf_op jit(solution)/shard_map/slice | solution.py:28
  441.6 3.0 slice_select_fusion
  444.6 0.3 maximum_select_fusion.1
  444.9 10.3 %fusion.1 = f32[1,3072,2048]{2,1,0:T(8,128)} fusion(f32[3072,1792]{1,0:T(8,128)S(1)} %slice.110, f32[3072,256]{1,0:T(8,128)S(1)} %slice_select_fusion, f32[256,2048]{1,0:T(8,128)S(1)} %maximum_select_fusion.1), kind=kLoop, calls=%fused_computation.5 | loop fusion | flops 31457280 | bytes 52428800 | tf_op jit(solution)/shard_map/broadcast_in_dim | solution.py:74
  455.2 4.4 reduce_sum.38
  459.6 9.0 %all-gather.1 = f32[512,256]{1,0:T(8,128)S(1)} all-gather(f32[256,256]{1,0:T(8,128)S(1)} %dynamic-slice_select_fusion), channel_id=3, replica_groups=mesh['grp'=4,'row'=4,'col'=2] {'col'}, dimensions={0}, use_global_device_ids=true | all-gather | bytes 786432 | tf_op jit(solution)/shard_map/all_gather | solution.py:12
  468.6 4.8 %convolution_subtract_fusion.1 = f32[256,2048]{1,0:T(8,128)} fusion(f32[256,2048]{1,0:T(8,128)} %param.3, f32[256,256]{1,0:T(8,128)S(1)} %reduce_sum.39, f32[256,2048]{1,0:T(8,128)S(1)} %reduce_sum.38), kind=kOutput, calls=%fused_computation.11 | convolution fusion | flops 1611137024 | bytes 6553600 | tf_op jit(solution)/shard_map/dot_general | solution.py:67
  (22 shorter events, 0.4 us)
Async XLA Ops:
  7.2 131.9 %all-gather.10.cloned.1.call-start = ((), (), s32[]{:S(2)}) async-start(), calls=%async_computation.2 | async-start | bytes 28311552 | tf_op jit(solution)/shard_map/all_gather | solution.py:12
  11.0 308.8 %all-gather.6.cloned.1.call-start = ((), (), s32[]{:S(2)}) async-start(), calls=%async_computation | async-start | bytes 11796480 | tf_op jit(solution)/shard_map/all_gather | solution.py:12
  148.6 4.3 copy-start.1
  152.9 302.3 %all-gather.8.cloned.1.call-start = ((), (), s32[]{:S(2)}) async-start(), calls=%async_computation.1 | async-start | bytes 10485760 | tf_op jit(solution)/shard_map/all_gather | solution.py:12
  364.7 0.7 copy-start.2
  403.2 1.5 copy-start
Sparse Core Ops, SparseCore 0:
  11.1 127.9 all-gather.9
  153.0 166.7 all-gather.5
  390.6 56.4 all-gather.7
